TPU v7x, 32 devices: a whole 2x2x4 slice. The times are simulated.
32 devices in a mesh: rep: 8 (over y, x, core), fsdp: 4 (over z).
Axes of the slice: x: 2, y: 2, z: 4, core: 2. Of those that a mesh axis runs over, the one named last changes fastest.
Arguments:
- queries: bfloat16 [4096, 4096], P(('rep', 'fsdp')), may hold values from -18 to 18
- resp_keys: bfloat16 [4096, 512], P(('rep', 'fsdp')), may hold values from -6 to 6
- resp_values: bfloat16 [4096, 512], P(('rep', 'fsdp')), may hold values from -6 to 6
- attn_out: bfloat16 [4096, 4096], P(('rep', 'fsdp')), may hold values from -1.796875 to 1.796875
- out_grad: bfloat16 [4096, 4096], P(('rep', 'fsdp')), may hold values from -24 to 24
- lengths: int32 [32], P(('rep', 'fsdp')), may hold values from 1 to 128, 2560 in all
- prefix_keys: bfloat16 [64, 512], P('fsdp'), may hold values from -18 to 18
- prefix_values: bfloat16 [64, 512], P('fsdp'), may hold values from -6 to 6
Outputs:
- query_grad: bfloat16 [4096, 4096], P(('rep', 'fsdp'))
- key_grad: bfloat16 [4096, 512], P(('rep', 'fsdp'))
- value_grad: bfloat16 [4096, 512], P(('rep', 'fsdp'))
- prefix_key_grad: float32 [64, 512], P('fsdp')
- prefix_value_grad: float32 [64, 512], P('fsdp')
Inputs may be any that keep to these rules, and one draw needn't show every extreme that they name: The largest of lengths is exactly 128.
All inputs are finite; a program needn't handle non-finite values. No bound on the sum of `lengths` on one device may be relied on, other than what follows from the above.
Results may differ from a plain program's by a relative error of at most 0.0078.
Values may be sent and summed in bfloat16 or wider, within the bound.
A program may use at most 64 MiB of HBM per device.

v0:
```python
import jax
import jax.numpy as jnp
from jax import lax
from jax.sharding import PartitionSpec as P

HEAD_DIM = 128
Q_HEADS = 32
KV_HEADS = 4


masked_fill = -1e30


def local_grads(
    queries, resp_keys, resp_values, attn_out, out_grad, length, prefix_keys, prefix_values
):
    resp_rows = queries.shape[0]
    prefix_rows = prefix_keys.shape[0]
    key_count = prefix_rows + resp_rows
    all_keys = jnp.concatenate([prefix_keys, resp_keys], axis=0)
    all_values = jnp.concatenate([prefix_values, resp_values], axis=0)
    row_index = jnp.arange(resp_rows, dtype=jnp.int32)[:, None]
    col_index = jnp.arange(key_count, dtype=jnp.int32)[None, :]
    live_rows = row_index < length
    visible = live_rows & ((col_index < prefix_rows) | (col_index - prefix_rows <= row_index))
    dead_rows = 1.0 - live_rows.astype(jnp.float32)
    group_size = Q_HEADS // KV_HEADS
    score_scale = HEAD_DIM ** (-0.5)
    block_width = group_size * HEAD_DIM
    query_parts = []
    key_parts = []
    value_parts = []
    for group_index in range(KV_HEADS):
        lower = group_index * block_width
        q_block = queries[:, lower : lower + block_width].reshape(resp_rows, group_size, HEAD_DIM)
        out_block = attn_out[:, lower : lower + block_width].reshape(
            resp_rows, group_size, HEAD_DIM
        )
        grad_block = out_grad[:, lower : lower + block_width].reshape(
            resp_rows, group_size, HEAD_DIM
        )
        key_block = all_keys[:, group_index * HEAD_DIM : (group_index + 1) * HEAD_DIM]
        value_block = all_values[:, group_index * HEAD_DIM : (group_index + 1) * HEAD_DIM]
        scores = (
            jnp.einsum("rhd,kd->hrk", q_block, key_block, preferred_element_type=jnp.float32)
            * score_scale
        )
        scores = jnp.where(visible[None], scores, masked_fill)
        row_max = jnp.max(scores, axis=2, keepdims=True)
        shifted = jnp.where(visible[None], jnp.exp(scores - row_max), 0.0)
        denominator = jnp.sum(shifted, axis=2, keepdims=True) + dead_rows[None]
        log_total = row_max + jnp.log(denominator)
        attn_prob = jnp.where(visible[None], jnp.exp(scores - log_total), 0.0)
        prob_half = attn_prob.astype(jnp.bfloat16)
        value_part = jnp.einsum(
            "hrk,rhd->kd", prob_half, grad_block, preferred_element_type=jnp.float32
        )
        prob_grad = jnp.einsum(
            "rhd,kd->hrk", grad_block, value_block, preferred_element_type=jnp.float32
        )
        row_delta = jnp.einsum(
            "rhd,rhd->hr", grad_block, out_block, preferred_element_type=jnp.float32
        )
        score_half = (attn_prob * (prob_grad - row_delta[:, :, None])).astype(jnp.bfloat16)
        query_part = (
            jnp.einsum("hrk,kd->rhd", score_half, key_block, preferred_element_type=jnp.float32)
            * score_scale
        )
        key_part = (
            jnp.einsum("hrk,rhd->kd", score_half, q_block, preferred_element_type=jnp.float32)
            * score_scale
        )
        query_parts.append(query_part.reshape(resp_rows, block_width))
        key_parts.append(key_part)
        value_parts.append(value_part)
    query_grad = jnp.concatenate(query_parts, axis=1).astype(jnp.bfloat16)
    key_whole = jnp.concatenate(key_parts, axis=1)
    value_whole = jnp.concatenate(value_parts, axis=1)
    return (query_grad, key_whole, value_whole)


def on_device(
    queries, resp_keys, resp_values, attn_out, out_grad, lengths, prefix_keys, prefix_values
):
    shared_keys, shared_values = (
        lax.all_gather(prefix_keys, "fsdp", axis=0, tiled=True),
        lax.all_gather(prefix_values, "fsdp", axis=0, tiled=True),
    )
    query_grad, key_whole, value_whole = local_grads(
        queries, resp_keys, resp_values, attn_out, out_grad, lengths[0], shared_keys, shared_values
    )
    prefix_rows = shared_keys.shape[0]
    prefix_key_part = key_whole[:prefix_rows]
    prefix_value_part = value_whole[:prefix_rows]
    within_keys, within_values = (
        lax.psum_scatter(prefix_key_part, "fsdp", scatter_dimension=0, tiled=True),
        lax.psum_scatter(prefix_value_part, "fsdp", scatter_dimension=0, tiled=True),
    )
    key_sums, value_sums = lax.psum((within_keys, within_values), "rep")
    key_grad = key_whole[prefix_rows:].astype(jnp.bfloat16)
    value_grad = value_whole[prefix_rows:].astype(jnp.bfloat16)
    return (query_grad, key_grad, value_grad, key_sums, value_sums)


def solution(mesh):
    in_specs = (
        P(("rep", "fsdp"), None),
        P(("rep", "fsdp"), None),
        P(("rep", "fsdp"), None),
        P(("rep", "fsdp"), None),
        P(("rep", "fsdp"), None),
        P(("rep", "fsdp")),
        P("fsdp", None),
        P("fsdp", None),
    )
    out_specs = (
        P(("rep", "fsdp"), None),
        P(("rep", "fsdp"), None),
        P(("rep", "fsdp"), None),
        P("fsdp", None),
        P("fsdp", None),
    )
    return jax.shard_map(
        on_device, mesh=mesh, in_specs=in_specs, out_specs=out_specs, check_vma=False
    )
```

profile of v0, /device:TPU:0, one launch (start us, length us, event | category | flops | bytes accessed | tf_op | source)
XLA Modules:
  0.0 165.2 jit_solution(2145563776102687001)
XLA Ops:
  7.9 15.1 %all_gather.6 = bf16[64,512]{1,0:T(8,128)(2,1)S(1)} all-gather(bf16[16,512]{1,0:T(8,128)(2,1)} %param.14), channel_id=1, replica_groups=mesh['rep'=8,'fsdp'=4] {'fsdp'}, dimensions={0}, use_global_device_ids=true | all-gather | bytes 81920 | tf_op jit(solution)/shard_map/all_gather | solution.py:86
  23.1 1.3 fusion.55
  24.3 0.9 copy.93
  27.4 1.1 fusion.58
  28.5 1.0 fusion.54
  29.5 1.1 copy.90
  30.6 1.8 %copy.94 = bf16[128,1024]{0,1:T(8,128)(2,1)} copy(bf16[128,1024]{1,0:T(8,128)(2,1)} %get-tuple-element.16) | data formatting | bytes 524288
  32.4 1.8 %copy.92 = bf16[128,1024]{0,1:T(8,128)(2,1)} copy(bf16[128,1024]{1,0:T(8,128)(2,1)} %get-tuple-element.17) | data formatting | bytes 524288
  34.2 1.8 %copy.96 = bf16[128,1024]{0,1:T(8,128)(2,1)} copy(bf16[128,1024]{1,0:T(8,128)(2,1)} %get-tuple-element.18) | data formatting | bytes 524288
  40.2 13.5 %all_gather.7 = bf16[64,512]{1,0:T(8,128)(2,1)S(1)} all-gather(bf16[16,512]{1,0:T(8,128)(2,1)} %param.15), channel_id=1, replica_groups=mesh['rep'=8,'fsdp'=4] {'fsdp'}, dimensions={0}, use_global_device_ids=true | all-gather | bytes 81920 | tf_op jit(solution)/shard_map/all_gather | solution.py:87
  54.4 1.3 slice_bitcast_fusion.3
  55.6 0.8 copy.97
  56.4 0.8 copy.98
  57.2 0.8 copy.100
  58.7 1.9 %copy.79 = f32[8,128,128]{2,0,1:T(8,128)} copy(bf16[8,128,128]{1,2,0:T(8,128)(2,1)} %bitcast.192) | data formatting | bytes 786432
  60.6 2.0 %multiply_reduce_fusion = f32[8,128]{0,1:T(8,128)} fusion(f32[8,128,128]{2,0,1:T(8,128)} %copy.79, bf16[128,8,128]{2,1,0:T(8,128)(2,1)} %bitcast.206), kind=kLoop, calls=%fused_computation.61 | loop fusion | flops 392192 | bytes 790528
  62.5 0.9 copy.80
  63.4 1.6 constant_dynamic-update-slice_fusion.2
  65.0 1.3 fusion.19
  67.1 0.9 fusion.24
  68.0 1.9 %copy.61 = f32[8,128,128]{2,0,1:T(8,128)} copy(bf16[8,128,128]{1,2,0:T(8,128)(2,1)} %bitcast.189) | data formatting | bytes 786432
  69.9 1.9 %multiply_reduce_fusion.2 = f32[8,128]{0,1:T(8,128)} fusion(f32[8,128,128]{2,0,1:T(8,128)} %copy.61, bf16[128,8,128]{2,1,0:T(8,128)(2,1)S(1)} %bitcast.205), kind=kLoop, calls=%fused_computation.63 | loop fusion | flops 392192 | bytes 790528
  71.8 0.9 copy.62
  72.7 1.2 fusion.17
  74.6 0.9 fusion.26
  76.0 1.1 fusion.18
  78.4 1.1 fusion.16
  82.3 1.0 pad_maximum_fusion
  83.4 17.9 %reduce-scatter.3.cloned.1.call-done = f32[16,512]{1,0:T(8,128)} async-done(((f32[64,512]{1,0:T(8,128)}), f32[16,512]{1,0:T(8,128)}) %reduce-scatter.3.cloned.1.call-update) | async-done | bytes 32784 | tf_op jit(solution)/shard_map/reduce_scatter | solution.py:96
  102.6 53.2 %all-reduce.3.cloned.1.call-done = (f32[16,512]{1,0:T(8,128)}, f32[16,512]{1,0:T(8,128)}) async-done(((f32[16,512]{1,0:T(8,128)}, f32[16,512]{1,0:T(8,128)}), (f32[16,512]{1,0:T(8,128)}, f32[16,512]{1,0:T(8,128)})) %all-reduce.3.cloned.1.call-update) | async-done | bytes 65552 | tf_op jit(solution)/shard_map/psum | solution.py:99
  155.9 1.4 copy.106
  157.3 1.4 copy.107
  (114 shorter events, 14.8 us)
Async XLA Ops:
  7.2 76.2 %reduce-scatter.5.cloned.1.call-start = ((), (), s32[]{:S(2)}) async-start(), calls=%async_computation.3 | async-start | bytes 163840 | tf_op jit(solution)/shard_map/reduce_scatter | solution.py:97
  24.3 1.4 copy-start.31
  25.4 1.4 copy-start.13
  25.5 1.2 copy-start.9
  25.8 1.0 copy-start.17
  26.4 0.9 copy-start.11
  26.7 1.7 %copy-start.19 = (bf16[128,4096]{1,0:T(8,128)(2,1)S(1)}, bf16[128,4096]{1,0:T(8,128)(2,1)}, u32[]{:S(2)}) copy-start(bf16[128,4096]{1,0:T(8,128)(2,1)} %param.12) | copy-start | bytes 3145732
  36.6 1.0 copy-start
  36.6 1.2 copy-start.2
  37.6 1.0 copy-start.4
  37.9 1.0 copy-start.23
  40.2 61.1 %reduce-scatter.3.cloned.1.call-start = ((), (), s32[]{:S(2)}) async-start(), calls=%async_computation.2 | async-start | bytes 163840 | tf_op jit(solution)/shard_map/reduce_scatter | solution.py:96
  63.4 3.7 %copy-start.16 = (bf16[128,1024]{0,1:T(8,128)(2,1)S(1)}, bf16[128,1024]{0,1:T(8,128)(2,1)}, u32[]{:S(2)}) copy-start(bf16[128,1024]{0,1:T(8,128)(2,1)} %copy-done.15) | copy-start | bytes 786436
  66.3 0.7 copy-start.5
  67.1 2.8 %copy-start.22 = (bf16[16,8,8,128]{3,2,1,0:T(8,128)(2,1)S(1)}, bf16[16,8,8,128]{3,2,1,0:T(8,128)(2,1)}, u32[]{:S(2)}) copy-start(bf16[16,8,8,128]{3,2,1,0:T(8,128)(2,1)} %copy.98) | copy-start | bytes 786436
  67.1 5.6 %copy-start.3 = (bf16[128,1024]{0,1:T(8,128)(2,1)S(1)}, bf16[128,1024]{0,1:T(8,128)(2,1)}, u32[]{:S(2)}) copy-start(bf16[128,1024]{0,1:T(8,128)(2,1)} %copy.92) | copy-start | bytes 786436
  69.9 4.7 %copy-start.14 = (bf16[128,1024]{0,1:T(8,128)(2,1)S(1)}, bf16[128,1024]{0,1:T(8,128)(2,1)}, u32[]{:S(2)}) copy-start(bf16[128,1024]{0,1:T(8,128)(2,1)} %copy-done.13) | copy-start | bytes 786436
  72.7 2.8 %copy-start.1 = (bf16[128,1024]{0,1:T(8,128)(2,1)S(1)}, bf16[128,1024]{0,1:T(8,128)(2,1)}, u32[]{:S(2)}) copy-start(bf16[128,1024]{0,1:T(8,128)(2,1)} %copy.94) | copy-start | bytes 786436
  73.8 0.7 copy-start.7
  74.6 1.1 copy-start.21
  75.7 1.4 copy-start.12
  77.1 1.0 copy-start.20
  78.1 1.4 copy-start.10
  78.4 1.5 copy-start.29
  78.4 1.5 copy-start.30
  79.5 1.1 copy-start.6
  79.5 1.1 copy-start.18
  79.5 1.3 copy-start.8
  80.5 75.3 %all-reduce.3.cloned.1.call-start = ((), (), s32[]{:S(2)}) async-start(), calls=%async_computation.4 | async-start | bytes 131072 | tf_op jit(solution)/shard_map/psum | solution.py:99
  82.3 1.1 copy-start.24
  82.3 1.1 copy-start.26
  82.3 1.1 copy-start.28
  (3 other events, 2.0 us)
Sparse Core Ops, SparseCore 0:
  40.3 20.5 reduce-scatter.4
  80.7 20.5 reduce-scatter.2
  104.4 51.4 all-reduce.2
where the time goes:
time: 166 us; the launch traced here: 165 us
  waiting for transfers between devices  71.2 us (43%)
  local copies, waits for them, and re-layouts  31.7 us (19%)
  blocking collectives  28.7 us (17%)
  between operations  15 us (9%)
  matrix products  11 us (7%)
  other arithmetic  7.5 us (5%)
    psum x1, waiting for transfers between devices, on_device(): key_sums, value_sums = lax.psum((within_keys, within_values), 'rep')  53.2 us
    unnamed x85, local copies, waits for them, and re-layouts  24 us
    reduce_scatter x1, waiting for transfers between devices, on_device(): lax.psum_scatter(prefix_key_part, 'fsdp', scatter_dimension=0, tiled=True)  17.9 us
    all_gather x1, blocking collectives, on_device(): lax.all_gather(prefix_keys, 'fsdp', axis=0, tiled=True)  15.1 us
    all_gather x1, blocking collectives, on_device(): lax.all_gather(prefix_values, 'fsdp', axis=0, tiled=True)  13.5 us
    dot_general x4, matrix products, local_grads(): jnp.einsum('rhd,kd->hrk', grad_block, value_block, preferred_element_type...  4.67 us
    unnamed x4, other arithmetic  4.3 us
  transfers between devices with their start and end apart: 3, of which 2 were waited for; matrix products, arithmetic and copies ran while one was open for 17% of the time, Pallas kernels for 0%

commit v1 on v0

v1 whole, which is shorter than its diff:
```python
import functools

import jax
import jax.numpy as jnp
from jax import lax
from jax.experimental import pallas as pl
from jax.experimental.pallas import tpu as pltpu
from jax.sharding import PartitionSpec as P

HEAD_DIM = 128
Q_HEADS = 32
KV_HEADS = 4
GROUP = Q_HEADS // KV_HEADS
WIDTH = GROUP * HEAD_DIM
SCALE = HEAD_DIM ** (-0.5)
MASKED = -1e30
LAG = 2
PAIR = 2

MESH = pl.DeviceIdType.MESH
F32 = jnp.float32
BF16 = jnp.bfloat16


def dot(a, b, contract):
    return lax.dot_general(a, b, (contract, ((), ())), preferred_element_type=F32)


def kernel(
    n_rep, n_fsdp,
    q_hbm, k_hbm, v_hbm, o_hbm, do_hbm, len_ref, pk_hbm, pv_hbm,
    qg_out, kg_out, vg_out, pk_out, pv_out,
    qb, ob, db, kb, vb, kvp, prob, score, zsend, zrecv, rbuf,
    in_sem, pre_sem, ag_send, ag_recv, z_ssem, z_rsem, r_ssem, r_rsem,
):
    rep, fs = lax.axis_index("rep"), lax.axis_index("fsdp")
    rows = qb.shape[1]
    pre_rows = kvp.shape[3]
    prefix = n_fsdp * pre_rows

    def rep_at(d):
        return lax.rem(rep + d, n_rep)

    def fs_at(d):
        return lax.rem(fs + d, n_fsdp)

    for i, src in enumerate((pk_hbm, pv_hbm)):
        for g in range(KV_HEADS):
            pltpu.make_async_copy(
                src.at[:, pl.ds(g * HEAD_DIM, HEAD_DIM)], kvp.at[fs, g, i], pre_sem.at[i, g]
            ).start()
    barrier = pltpu.get_barrier_semaphore()
    for d in range(1, n_fsdp):
        pl.semaphore_signal(barrier, inc=1, device_id=(rep, fs_at(d)), device_id_type=MESH)
    for d in range(1, n_rep):
        pl.semaphore_signal(barrier, inc=1, device_id=(rep_at(d), fs), device_id_type=MESH)
    loads = ((q_hbm, qb, WIDTH), (do_hbm, db, WIDTH), (o_hbm, ob, WIDTH),
             (k_hbm, kb, HEAD_DIM), (v_hbm, vb, HEAD_DIM))
    for g in range(KV_HEADS):
        for i, (src, dst, width) in enumerate(loads):
            pltpu.make_async_copy(
                src.at[:, pl.ds(g * width, width)], dst.at[g], in_sem.at[g, i]
            ).start()
    for i in range(2):
        for g in range(KV_HEADS):
            pltpu.make_async_copy(kvp.at[fs, g, i], kvp.at[fs, g, i], pre_sem.at[i, g]).wait()
    pl.semaphore_wait(barrier, n_fsdp + n_rep - 2)

    def gather(d):
        return pltpu.make_async_remote_copy(
            src_ref=kvp.at[fs], dst_ref=kvp.at[fs], send_sem=ag_send.at[d - 1],
            recv_sem=ag_recv.at[d - 1], device_id=(rep, fs_at(d)), device_id_type=MESH)

    def scatter(g, d):
        return pltpu.make_async_remote_copy(
            src_ref=zsend.at[g, fs_at(d)], dst_ref=zrecv.at[g, fs], send_sem=z_ssem.at[g, d - 1],
            recv_sem=z_rsem.at[g, d - 1], device_id=(rep, fs_at(d)), device_id_type=MESH)

    def spread(g, d):
        return pltpu.make_async_remote_copy(
            src_ref=rbuf.at[g, rep], dst_ref=rbuf.at[g, rep], send_sem=r_ssem.at[g, d - 1],
            recv_sem=r_rsem.at[g, d - 1], device_id=(rep_at(d), fs), device_id_type=MESH)

    for d in range(1, n_fsdp):
        gather(d).start()

    length = len_ref[0]
    lanes = PAIR * HEAD_DIM if rows == HEAD_DIM else PAIR * rows
    lane = lax.broadcasted_iota(jnp.int32, (rows, lanes), 1)
    pos = lax.rem(lane, rows)
    causal = lax.broadcasted_iota(jnp.int32, (rows, lanes), 0) <= pos
    live = lax.rem(lax.broadcasted_iota(jnp.int32, (1, lanes), 1), rows) < length
    low_half = lax.broadcasted_iota(jnp.int32, (lanes, HEAD_DIM), 1) < HEAD_DIM // 2
    minus = jnp.full((prefix + rows, HEAD_DIM), -1.0, BF16)

    for d in range(1, n_fsdp):
        own = kvp.at[fs_at(n_fsdp - d)]
        pltpu.make_async_copy(own, own, ag_recv.at[d - 1]).wait()

    def reduce_rows(g):
        for d in range(1, n_fsdp):
            slot = zrecv.at[g, fs_at(n_fsdp - d)]
            pltpu.make_async_copy(slot, slot, z_rsem.at[g, d - 1]).wait()
        zrecv[g, fs] = zsend[g, fs]
        total = zrecv[g, 0]
        for i in range(1, n_fsdp):
            total = total + zrecv[g, i]
        rbuf[g, rep] = total
        for d in range(1, n_rep):
            spread(g, d).start()

    def group(g, carry):
        for i, (_, dst, _) in enumerate(loads):
            pltpu.make_async_copy(dst.at[g], dst.at[g], in_sem.at[g, i]).wait()
        keys = jnp.concatenate([kvp[:, g, 0].reshape(prefix, HEAD_DIM), kb[g]], axis=0)
        values = jnp.concatenate([kvp[:, g, 1].reshape(prefix, HEAD_DIM), vb[g]], axis=0)
        values_ext = jnp.concatenate([values, minus], axis=1)

        def heads(ref, first, count):
            return jnp.concatenate(
                [ref[g, :, h * HEAD_DIM:(h + 1) * HEAD_DIM] for h in range(first, first + count)],
                axis=0)

        for c in range(GROUP // PAIR):
            q = heads(qb, c * PAIR, PAIR)
            do = heads(db, c * PAIR, PAIR)
            o = heads(ob, c * PAIR, PAIR)
            prod = do.astype(F32) * o.astype(F32)
            both = prod + pltpu.roll(prod, HEAD_DIM // 2, 1)
            rest = both - both.astype(BF16).astype(F32)
            delta = jnp.where(low_half, both, rest).astype(BF16)
            s = dot(keys, q, ((1,), (1,)))
            dp = dot(values_ext, jnp.concatenate([do, delta], axis=1), ((1,), (1,)))
            s = jnp.concatenate(
                [s[:prefix], jnp.where(causal, s[prefix:], MASKED)], axis=0)
            top = jnp.max(s, axis=0, keepdims=True)
            e = jnp.exp((s - top) * SCALE)
            inv = jnp.where(live, 1.0 / jnp.sum(e, axis=0, keepdims=True), 0.0)
            p = e * inv
            prob[:, c * lanes:(c + 1) * lanes] = p.astype(BF16)
            ds = (p * dp).astype(BF16)
            score[:, c * lanes:(c + 1) * lanes] = ds
            dq = (dot(ds, keys, ((0,), (0,))) * SCALE).astype(BF16)
            for j in range(PAIR):
                at = pl.multiple_of(g * WIDTH + (c * PAIR + j) * HEAD_DIM, HEAD_DIM)
                qg_out[:, pl.ds(at, HEAD_DIM)] = dq[j * rows:(j + 1) * rows]
        dv = dot(prob[...], heads(db, 0, GROUP), ((1,), (0,)))
        dk = dot(score[...], heads(qb, 0, GROUP), ((1,), (0,))) * SCALE
        zsend[g, :, 0] = dk[:prefix].reshape(n_fsdp, pre_rows, HEAD_DIM)
        zsend[g, :, 1] = dv[:prefix].reshape(n_fsdp, pre_rows, HEAD_DIM)
        for d in range(1, n_fsdp):
            scatter(g, d).start()
        at = pl.multiple_of(g * HEAD_DIM, HEAD_DIM)
        kg_out[:, pl.ds(at, HEAD_DIM)] = dk[prefix:].astype(BF16)
        vg_out[:, pl.ds(at, HEAD_DIM)] = dv[prefix:].astype(BF16)

        @pl.when(g >= LAG)
        def _():
            reduce_rows(g - LAG)

        return carry

    lax.fori_loop(0, KV_HEADS, group, 0)
    for g in range(KV_HEADS - LAG, KV_HEADS):
        reduce_rows(g)
    for g in range(KV_HEADS):
        for d in range(1, n_rep):
            slot = rbuf.at[g, rep_at(n_rep - d)]
            pltpu.make_async_copy(slot, slot, r_rsem.at[g, d - 1]).wait()
        total = rbuf[g, 0]
        for i in range(1, n_rep):
            total = total + rbuf[g, i]
        pk_out[:, g * HEAD_DIM:(g + 1) * HEAD_DIM] = total[0]
        pv_out[:, g * HEAD_DIM:(g + 1) * HEAD_DIM] = total[1]
    for d in range(1, n_fsdp):
        gather(d).wait_send()
    for g in range(KV_HEADS):
        for d in range(1, n_fsdp):
            scatter(g, d).wait_send()
        for d in range(1, n_rep):
            spread(g, d).wait_send()


def on_device(n_rep, n_fsdp, q, k, v, o, do, lengths, pk, pv):
    rows = q.shape[0]
    pre_rows = pk.shape[0]
    keys = n_fsdp * pre_rows + rows
    any_ = pl.BlockSpec(memory_space=pl.ANY)
    vmem = pl.BlockSpec(memory_space=pltpu.VMEM)
    dma = pltpu.SemaphoreType.DMA
    piece = (2, pre_rows, HEAD_DIM)
    return pl.pallas_call(
        functools.partial(kernel, n_rep, n_fsdp),
        out_shape=(
            jax.ShapeDtypeStruct(q.shape, BF16),
            jax.ShapeDtypeStruct(k.shape, BF16),
            jax.ShapeDtypeStruct(v.shape, BF16),
            jax.ShapeDtypeStruct(pk.shape, F32),
            jax.ShapeDtypeStruct(pv.shape, F32),
        ),
        in_specs=[any_] * 5 + [pl.BlockSpec(memory_space=pltpu.SMEM)] + [any_] * 2,
        out_specs=(vmem,) * 5,
        scratch_shapes=[
            pltpu.VMEM((KV_HEADS, rows, WIDTH), BF16),
            pltpu.VMEM((KV_HEADS, rows, WIDTH), BF16),
            pltpu.VMEM((KV_HEADS, rows, WIDTH), BF16),
            pltpu.VMEM((KV_HEADS, rows, HEAD_DIM), BF16),
            pltpu.VMEM((KV_HEADS, rows, HEAD_DIM), BF16),
            pltpu.VMEM((n_fsdp, KV_HEADS) + piece, BF16),
            pltpu.VMEM((keys, GROUP * rows), BF16),
            pltpu.VMEM((keys, GROUP * rows), BF16),
            pltpu.VMEM((KV_HEADS, n_fsdp) + piece, F32),
            pltpu.VMEM((KV_HEADS, n_fsdp) + piece, F32),
            pltpu.VMEM((KV_HEADS, n_rep) + piece, F32),
            dma((KV_HEADS, 5)),
            dma((2, KV_HEADS)),
            dma((n_fsdp - 1,)),
            dma((n_fsdp - 1,)),
            dma((KV_HEADS, n_fsdp - 1)),
            dma((KV_HEADS, n_fsdp - 1)),
            dma((KV_HEADS, n_rep - 1)),
            dma((KV_HEADS, n_rep - 1)),
        ],
        compiler_params=pltpu.CompilerParams(collective_id=0, has_side_effects=True),
    )(q, k, v, o, do, lengths, pk, pv)


def solution(mesh):
    wide = P(("rep", "fsdp"), None)
    return jax.shard_map(
        functools.partial(on_device, mesh.shape["rep"], mesh.shape["fsdp"]),
        mesh=mesh,
        in_specs=(wide,) * 5 + (P(("rep", "fsdp")), P("fsdp", None), P("fsdp", None)),
        out_specs=(wide,) * 3 + (P("fsdp", None), P("fsdp", None)),
        check_vma=False,
    )
```

time: 166 us -> 33.5 us (0.20)
  waiting for transfers between devices: 71.2 us -> 0 us
  blocking collectives: 28.7 us -> 0 us
  Pallas kernels: 0 us -> 26.5 us
  local copies, waits for them, and re-layouts: 31.7 us -> 5.42 us
  between operations: 15 us -> 1.3 us
  matrix products: 11 us -> 0 us
  other arithmetic: 7.5 us -> 0 us
    psum x1 -> x0, waiting for transfers between devices: 53.2 us -> none  [on_device(): key_sums, value_sums = lax.psum((within_keys, within_values), 'rep')]
    all_gather x2 -> x0, blocking collectives: 28.7 us -> none  [the longest x1 15.1 us: on_device(): lax.all_gather(prefix_keys, 'fsdp', axis=0, tiled=True)]
    pallas_call x0 -> x1, Pallas kernels: none -> 26.5 us  [on_device(): pl.pallas_call(functools.partial(kernel, n_rep, n_fsdp), out_shape=(jax.S...]
    unnamed x85 -> x13, local copies, waits for them, and re-layouts: 24 us -> 5.42 us
    reduce_scatter x2 -> x0, waiting for transfers between devices: 17.9 us -> none  [the longest x1 17.9 us: on_device(): lax.psum_scatter(prefix_key_part, 'fsdp', scatter_dimension=0, tiled=True)]
    dot_general x20 -> x0, matrix products: 11 us -> none  [the longest x4 4.67 us: local_grads(): jnp.einsum('rhd,kd->hrk', grad_block, value_block, preferred_element_type...]
    unnamed x4 -> x0, other arithmetic: 4.3 us -> none
    slice x4 -> x0, local copies, waits for them, and re-layouts: 3.6 us -> none  [the longest x1 1.26 us: local_grads(): queries[:, lower:lower + block_width]]
  transfers between devices with their start and end apart: 3 -> 0, of which waited for: 2 -> 0; matrix products, arithmetic and copies ran while one was open for 17% -> 0% of each run, Pallas kernels for 0% -> 0%
where the time goes in v1:
time: 33.5 us; the launch traced here: 33.2 us
  Pallas kernels  26.5 us (79%)
  local copies, waits for them, and re-layouts  5.42 us (16%)
  between operations  1.3 us (4%)
    pallas_call x1, Pallas kernels, on_device(): pl.pallas_call(functools.partial(kernel, n_rep, n_fsdp), out_shape=(jax.S...  26.5 us
    unnamed x13, local copies, waits for them, and re-layouts  5.42 us

profile of v1, /device:TPU:0, one launch (start us, length us, event | category | flops | bytes accessed | tf_op | source)
XLA Modules:
  0.0 33.2 jit_solution(12707344466142977696)
XLA Ops:
  1.3 26.5 %shard_map.119 = (bf16[128,4096]{1,0:T(8,128)(2,1)}, bf16[128,512]{1,0:T(8,128)(2,1)}, bf16[128,512]{1,0:T(8,128)(2,1)}, f32[16,512]{1,0:T(8,128)}, f32[16,512]{1,0:T(8,128)}) custom-call(bf16[128,4096]{1,0:T(8,128)(2,1)} %q_hbm.1, bf16[128,512]{1,0:T(8,128)(2,1)} %k_hbm.1, bf16[128,512]{1,0:T(8,128)(2,1)} %v_hbm.1, bf16[128,4096]{1,0:T(8,128)(2,1)} %o_hbm.1, ...), custom_call_target="tpu_custom_call" | custom-call | tf_op jit(solution)/shard_map/pallas_call | solution.py:192
  27.8 0.0 copy-start.1
  27.8 2.3 %copy.19 = bf16[128,4096]{1,0:T(8,128)(2,1)} copy(bf16[128,4096]{1,0:T(8,128)(2,1)} %get-tuple-element.10) | data formatting | bytes 2097152
  30.1 0.0 copy-done.1
  30.1 0.0 copy-start
  30.1 0.7 %copy.20 = bf16[128,512]{1,0:T(8,128)(2,1)} copy(bf16[128,512]{1,0:T(8,128)(2,1)S(1)} %copy-done.1) | data formatting | bytes 262144
  30.8 0.3 copy-done
  31.1 0.0 copy-start.3
  31.1 0.7 %copy.21 = bf16[128,512]{1,0:T(8,128)(2,1)} copy(bf16[128,512]{1,0:T(8,128)(2,1)S(1)} %copy-done) | data formatting | bytes 262144
  31.7 0.1 copy-done.3
  31.8 0.0 copy-start.2
  31.8 0.6 %copy.22 = f32[16,512]{1,0:T(8,128)} copy(f32[16,512]{1,0:T(8,128)S(1)} %copy-done.3) | data formatting | bytes 65536
  32.4 0.2 copy-done.2
  32.6 0.6 %copy.23 = f32[16,512]{1,0:T(8,128)} copy(f32[16,512]{1,0:T(8,128)S(1)} %copy-done.2) | data formatting | bytes 65536
Async XLA Ops:
  27.8 2.3 %copy-start.1 = (bf16[128,512]{1,0:T(8,128)(2,1)S(1)}, bf16[128,512]{1,0:T(8,128)(2,1)}, u32[]{:S(2)}) copy-start(bf16[128,512]{1,0:T(8,128)(2,1)} %get-tuple-element.11) | copy-start | bytes 393220
  30.1 1.0 %copy-start = (bf16[128,512]{1,0:T(8,128)(2,1)S(1)}, bf16[128,512]{1,0:T(8,128)(2,1)}, u32[]{:S(2)}) copy-start(bf16[128,512]{1,0:T(8,128)(2,1)} %get-tuple-element.12) | copy-start | bytes 393220
  31.1 0.8 %copy-start.3 = (f32[16,512]{1,0:T(8,128)S(1)}, f32[16,512]{1,0:T(8,128)}, u32[]{:S(2)}) copy-start(f32[16,512]{1,0:T(8,128)} %get-tuple-element.13) | copy-start | bytes 98308
  31.8 0.8 %copy-start.2 = (f32[16,512]{1,0:T(8,128)S(1)}, f32[16,512]{1,0:T(8,128)}, u32[]{:S(2)}) copy-start(f32[16,512]{1,0:T(8,128)} %get-tuple-element.14) | copy-start | bytes 98308

commit v2 on v1

--- a/solution.py
+++ b/solution.py
@@ -181,6 +181,15 @@
             spread(g, d).wait_send()
 
 
+def write_out(*refs):
+    sems = refs[-1]
+    copies = [pltpu.make_async_copy(refs[i], refs[5 + i], sems.at[i]) for i in range(5)]
+    for copy in copies:
+        copy.start()
+    for copy in copies:
+        copy.wait()
+
+
 def on_device(n_rep, n_fsdp, q, k, v, o, do, lengths, pk, pv):
     rows = q.shape[0]
     pre_rows = pk.shape[0]
@@ -189,14 +198,14 @@
     vmem = pl.BlockSpec(memory_space=pltpu.VMEM)
     dma = pltpu.SemaphoreType.DMA
     piece = (2, pre_rows, HEAD_DIM)
-    return pl.pallas_call(
+    held = pl.pallas_call(
         functools.partial(kernel, n_rep, n_fsdp),
         out_shape=(
-            jax.ShapeDtypeStruct(q.shape, BF16),
-            jax.ShapeDtypeStruct(k.shape, BF16),
-            jax.ShapeDtypeStruct(v.shape, BF16),
-            jax.ShapeDtypeStruct(pk.shape, F32),
-            jax.ShapeDtypeStruct(pv.shape, F32),
+            pltpu.VMEM(q.shape, BF16),
+            pltpu.VMEM(k.shape, BF16),
+            pltpu.VMEM(v.shape, BF16),
+            pltpu.VMEM(pk.shape, F32),
+            pltpu.VMEM(pv.shape, F32),
         ),
         in_specs=[any_] * 5 + [pl.BlockSpec(memory_space=pltpu.SMEM)] + [any_] * 2,
         out_specs=(vmem,) * 5,
@@ -223,6 +232,13 @@
         ],
         compiler_params=pltpu.CompilerParams(collective_id=0, has_side_effects=True),
     )(q, k, v, o, do, lengths, pk, pv)
+    return pl.pallas_call(
+        write_out,
+        out_shape=tuple(jax.ShapeDtypeStruct(x.shape, x.dtype) for x in held),
+        in_specs=[vmem] * 5,
+        out_specs=(any_,) * 5,
+        scratch_shapes=[dma((5,))],
+    )(*[pltpu.with_memory_space_constraint(x, pltpu.VMEM) for x in held])
 
 
 def solution(mesh):

time: 33.5 us -> 28 us (0.84)
  local copies, waits for them, and re-layouts: 5.42 us -> 0 us
    unnamed x13 -> x0, local copies, waits for them, and re-layouts: 5.42 us -> none
    pallas_call x1 -> x2, Pallas kernels: 26.5 us -> 26.5 us  [the longest x1 25.4 us: on_device(): pl.pallas_call(functools.partial(kernel, n_rep, n_fsdp), out_shape=(pltpu...]
where the time goes in v2:
time: 28 us; the launch traced here: 27.8 us
  Pallas kernels  26.5 us (95%)
  between operations  1.29 us (5%)
    pallas_call x1, Pallas kernels, on_device(): pl.pallas_call(functools.partial(kernel, n_rep, n_fsdp), out_shape=(pltpu...  25.4 us
    pallas_call x1, Pallas kernels, on_device(): pl.pallas_call(write_out, out_shape=tuple((jax.ShapeDtypeStruct(x.shape,...  1.1 us

profile of v2, /device:TPU:0, one launch (start us, length us, event | category | flops | bytes accessed | tf_op | source)
XLA Modules:
  0.0 27.8 jit_solution(5385694124507189610)
XLA Ops:
  1.3 25.4 %shard_map.119 = (bf16[128,4096]{1,0:T(8,128)(2,1)S(1)}, bf16[128,512]{1,0:T(8,128)(2,1)S(1)}, bf16[128,512]{1,0:T(8,128)(2,1)S(1)}, f32[16,512]{1,0:T(8,128)S(1)}, f32[16,512]{1,0:T(8,128)S(1)}) custom-call(bf16[128,4096]{1,0:T(8,128)(2,1)} %q_hbm.1, bf16[128,512]{1,0:T(8,128)(2,1)} %k_hbm.1, bf16[128,512]{1,0:T(8,128)(2,1)} %v_hbm.1, ...), custom_call_target="tpu_custom_call" | custom-call | tf_op jit(solution)/shard_map/pallas_call | solution.py:201
  26.7 1.1 %shard_map.120 = (bf16[128,4096]{1,0:T(8,128)(2,1)}, bf16[128,512]{1,0:T(8,128)(2,1)}, bf16[128,512]{1,0:T(8,128)(2,1)}, f32[16,512]{1,0:T(8,128)}, f32[16,512]{1,0:T(8,128)}) custom-call(bf16[128,4096]{1,0:T(8,128)(2,1)S(1)} %get-tuple-element.10.refs_0_, bf16[128,512]{1,0:T(8,128)(2,1)S(1)} %get-tuple-element.11.refs_1_, ...), custom_call_target="tpu_custom_call" | custom-call | tf_op jit(solution)/shard_map/pallas_call | solution.py:235

commit v3 on v2

--- a/solution.py
+++ b/solution.py
@@ -14,7 +14,6 @@
 WIDTH = GROUP * HEAD_DIM
 SCALE = HEAD_DIM ** (-0.5)
 MASKED = -1e30
-LAG = 2
 PAIR = 2
 
 MESH = pl.DeviceIdType.MESH
@@ -30,13 +29,15 @@
     n_rep, n_fsdp,
     q_hbm, k_hbm, v_hbm, o_hbm, do_hbm, len_ref, pk_hbm, pv_hbm,
     qg_out, kg_out, vg_out, pk_out, pv_out,
-    qb, ob, db, kb, vb, kvp, prob, score, zsend, zrecv, rbuf,
-    in_sem, pre_sem, ag_send, ag_recv, z_ssem, z_rsem, r_ssem, r_rsem,
+    qb, ob, db, kb, vb, kvp, own_e, own_dp, delta_b, stats, prob, score,
+    part, pairb, zsend, zrecv, rbuf,
+    in_sem, pre_sem, ag_send, ag_recv, p_ssem, p_rsem, z_ssem, z_rsem, r_ssem, r_rsem,
 ):
     rep, fs = lax.axis_index("rep"), lax.axis_index("fsdp")
     rows = qb.shape[1]
     pre_rows = kvp.shape[3]
     prefix = n_fsdp * pre_rows
+    kind = lax.rem(rep, 2)
 
     def rep_at(d):
         return lax.rem(rep + d, n_rep)
@@ -71,6 +72,11 @@
             src_ref=kvp.at[fs], dst_ref=kvp.at[fs], send_sem=ag_send.at[d - 1],
             recv_sem=ag_recv.at[d - 1], device_id=(rep, fs_at(d)), device_id_type=MESH)
 
+    def swap(g):
+        return pltpu.make_async_remote_copy(
+            src_ref=part.at[g, 1 - kind], dst_ref=pairb.at[g], send_sem=p_ssem.at[g],
+            recv_sem=p_rsem.at[g], device_id=(rep + 1 - 2 * kind, fs), device_id_type=MESH)
+
     def scatter(g, d):
         return pltpu.make_async_remote_copy(
             src_ref=zsend.at[g, fs_at(d)], dst_ref=zrecv.at[g, fs], send_sem=z_ssem.at[g, d - 1],
@@ -85,19 +91,55 @@
         gather(d).start()
 
     length = len_ref[0]
-    lanes = PAIR * HEAD_DIM if rows == HEAD_DIM else PAIR * rows
-    lane = lax.broadcasted_iota(jnp.int32, (rows, lanes), 1)
-    pos = lax.rem(lane, rows)
+    lanes = PAIR * rows
+    pos = lax.rem(lax.broadcasted_iota(jnp.int32, (rows, lanes), 1), rows)
     causal = lax.broadcasted_iota(jnp.int32, (rows, lanes), 0) <= pos
     live = lax.rem(lax.broadcasted_iota(jnp.int32, (1, lanes), 1), rows) < length
     low_half = lax.broadcasted_iota(jnp.int32, (lanes, HEAD_DIM), 1) < HEAD_DIM // 2
-    minus = jnp.full((prefix + rows, HEAD_DIM), -1.0, BF16)
+
+    def heads(ref, g, first, count):
+        return jnp.concatenate(
+            [ref[g, :, h * HEAD_DIM:(h + 1) * HEAD_DIM] for h in range(first, first + count)],
+            axis=0)
+
+    def own_keys(g, carry):
+        for i, (_, dst, _) in enumerate(loads):
+            pltpu.make_async_copy(dst.at[g], dst.at[g], in_sem.at[g, i]).wait()
+        keys = kb[g]
+        values = jnp.concatenate([vb[g], jnp.full((rows, HEAD_DIM), -1.0, BF16)], axis=1)
+        for c in range(GROUP // PAIR):
+            at = slice(c * lanes, (c + 1) * lanes)
+            q = heads(qb, g, c * PAIR, PAIR)
+            do = heads(db, g, c * PAIR, PAIR)
+            o = heads(ob, g, c * PAIR, PAIR)
+            prod = do.astype(F32) * o.astype(F32)
+            both = prod + pltpu.roll(prod, HEAD_DIM // 2, 1)
+            rest = both - both.astype(BF16).astype(F32)
+            delta = jnp.where(low_half, both, rest).astype(BF16)
+            delta_b[g, at] = delta
+            s = jnp.where(causal, dot(keys, q, ((1,), (1,))), MASKED)
+            top = jnp.max(s, axis=0, keepdims=True)
+            e = jnp.exp((s - top) * SCALE)
+            own_e[g, :, at] = e
+            stats[g, 0:1, at] = top
+            stats[g, 1:2, at] = jnp.sum(e, axis=0, keepdims=True)
+            own_dp[g, :, at] = dot(
+                values, jnp.concatenate([do, delta], axis=1), ((1,), (1,)))
+        return carry
+
+    lax.fori_loop(0, KV_HEADS, own_keys, 0)
 
     for d in range(1, n_fsdp):
-        own = kvp.at[fs_at(n_fsdp - d)]
-        pltpu.make_async_copy(own, own, ag_recv.at[d - 1]).wait()
-
-    def reduce_rows(g):
+        slot = kvp.at[fs_at(n_fsdp - d)]
+        pltpu.make_async_copy(slot, slot, ag_recv.at[d - 1]).wait()
+
+    def add_pair(g):
+        pltpu.make_async_copy(pairb.at[g], pairb.at[g], p_rsem.at[g]).wait()
+        zsend[g] = part[g, kind] + pairb[g]
+        for d in range(1, n_fsdp):
+            scatter(g, d).start()
+
+    def add_rows(g):
         for d in range(1, n_fsdp):
             slot = zrecv.at[g, fs_at(n_fsdp - d)]
             pltpu.make_async_copy(slot, slot, z_rsem.at[g, d - 1]).wait()
@@ -109,72 +151,84 @@
         for d in range(1, n_rep):
             spread(g, d).start()
 
-    def group(g, carry):
-        for i, (_, dst, _) in enumerate(loads):
-            pltpu.make_async_copy(dst.at[g], dst.at[g], in_sem.at[g, i]).wait()
+    def prefix_keys(g, carry):
+        keys = kvp[:, g, 0].reshape(prefix, HEAD_DIM)
+        values = jnp.concatenate(
+            [kvp[:, g, 1].reshape(prefix, HEAD_DIM), jnp.full((prefix, HEAD_DIM), -1.0, BF16)],
+            axis=1)
+        for c in range(GROUP // PAIR):
+            at = slice(c * lanes, (c + 1) * lanes)
+            q = heads(qb, g, c * PAIR, PAIR)
+            do = heads(db, g, c * PAIR, PAIR)
+            s = dot(keys, q, ((1,), (1,)))
+            dp = dot(values, jnp.concatenate([do, delta_b[g, at]], axis=1), ((1,), (1,)))
+            own_top = stats[g, 0:1, at]
+            top = jnp.maximum(jnp.max(s, axis=0, keepdims=True), own_top)
+            e = jnp.exp((s - top) * SCALE)
+            shrink = jnp.exp((own_top - top) * SCALE)
+            total = jnp.sum(e, axis=0, keepdims=True) + stats[g, 1:2, at] * shrink
+            inv = jnp.where(live, 1.0 / total, 0.0)
+            p = e * inv
+            stats[g, 2:3, at] = shrink * inv
+            prob[g, :prefix, at] = p.astype(BF16)
+            score[g, :prefix, at] = (p * dp).astype(BF16)
+        dk = dot(score[g, :prefix], heads(qb, g, 0, GROUP), ((1,), (0,))) * SCALE
+        dv = dot(prob[g, :prefix], heads(db, g, 0, GROUP), ((1,), (0,)))
+        part[g, 0] = dk.reshape(n_fsdp, pre_rows, HEAD_DIM)
+        part[g, 1] = dv.reshape(n_fsdp, pre_rows, HEAD_DIM)
+        swap(g).start()
+
+        @pl.when(g >= 1)
+        def _():
+            add_pair(g - 1)
+
+        return carry
+
+    lax.fori_loop(0, KV_HEADS, prefix_keys, 0)
+
+    def own_grads(g, carry):
         keys = jnp.concatenate([kvp[:, g, 0].reshape(prefix, HEAD_DIM), kb[g]], axis=0)
-        values = jnp.concatenate([kvp[:, g, 1].reshape(prefix, HEAD_DIM), vb[g]], axis=0)
-        values_ext = jnp.concatenate([values, minus], axis=1)
-
-        def heads(ref, first, count):
-            return jnp.concatenate(
-                [ref[g, :, h * HEAD_DIM:(h + 1) * HEAD_DIM] for h in range(first, first + count)],
-                axis=0)
-
         for c in range(GROUP // PAIR):
-            q = heads(qb, c * PAIR, PAIR)
-            do = heads(db, c * PAIR, PAIR)
-            o = heads(ob, c * PAIR, PAIR)
-            prod = do.astype(F32) * o.astype(F32)
-            both = prod + pltpu.roll(prod, HEAD_DIM // 2, 1)
-            rest = both - both.astype(BF16).astype(F32)
-            delta = jnp.where(low_half, both, rest).astype(BF16)
-            s = dot(keys, q, ((1,), (1,)))
-            dp = dot(values_ext, jnp.concatenate([do, delta], axis=1), ((1,), (1,)))
-            s = jnp.concatenate(
-                [s[:prefix], jnp.where(causal, s[prefix:], MASKED)], axis=0)
-            top = jnp.max(s, axis=0, keepdims=True)
-            e = jnp.exp((s - top) * SCALE)
-            inv = jnp.where(live, 1.0 / jnp.sum(e, axis=0, keepdims=True), 0.0)
-            p = e * inv
-            prob[:, c * lanes:(c + 1) * lanes] = p.astype(BF16)
-            ds = (p * dp).astype(BF16)
-            score[:, c * lanes:(c + 1) * lanes] = ds
-            dq = (dot(ds, keys, ((0,), (0,))) * SCALE).astype(BF16)
+            at = slice(c * lanes, (c + 1) * lanes)
+            p = own_e[g, :, at] * stats[g, 2:3, at]
+            prob[g, prefix:, at] = p.astype(BF16)
+            score[g, prefix:, at] = (p * own_dp[g, :, at]).astype(BF16)
+            dq = (dot(score[g, :, at], keys, ((0,), (0,))) * SCALE).astype(BF16)
             for j in range(PAIR):
-                at = pl.multiple_of(g * WIDTH + (c * PAIR + j) * HEAD_DIM, HEAD_DIM)
-                qg_out[:, pl.ds(at, HEAD_DIM)] = dq[j * rows:(j + 1) * rows]
-        dv = dot(prob[...], heads(db, 0, GROUP), ((1,), (0,)))
-        dk = dot(score[...], heads(qb, 0, GROUP), ((1,), (0,))) * SCALE
-        zsend[g, :, 0] = dk[:prefix].reshape(n_fsdp, pre_rows, HEAD_DIM)
-        zsend[g, :, 1] = dv[:prefix].reshape(n_fsdp, pre_rows, HEAD_DIM)
-        for d in range(1, n_fsdp):
-            scatter(g, d).start()
-        at = pl.multiple_of(g * HEAD_DIM, HEAD_DIM)
-        kg_out[:, pl.ds(at, HEAD_DIM)] = dk[prefix:].astype(BF16)
-        vg_out[:, pl.ds(at, HEAD_DIM)] = dv[prefix:].astype(BF16)
-
-        @pl.when(g >= LAG)
+                to = pl.multiple_of(g * WIDTH + (c * PAIR + j) * HEAD_DIM, HEAD_DIM)
+                qg_out[:, pl.ds(to, HEAD_DIM)] = dq[j * rows:(j + 1) * rows]
+        dk = dot(score[g, prefix:], heads(qb, g, 0, GROUP), ((1,), (0,))) * SCALE
+        dv = dot(prob[g, prefix:], heads(db, g, 0, GROUP), ((1,), (0,)))
+        to = pl.multiple_of(g * HEAD_DIM, HEAD_DIM)
+        kg_out[:, pl.ds(to, HEAD_DIM)] = dk.astype(BF16)
+        vg_out[:, pl.ds(to, HEAD_DIM)] = dv.astype(BF16)
+
+        @pl.when(g == 0)
         def _():
-            reduce_rows(g - LAG)
+            add_pair(KV_HEADS - 1)
+
+        @pl.when((g >= 1) & (g <= KV_HEADS // 2))
+        def _():
+            add_rows(2 * g - 2)
+            add_rows(2 * g - 1)
 
         return carry
 
-    lax.fori_loop(0, KV_HEADS, group, 0)
-    for g in range(KV_HEADS - LAG, KV_HEADS):
-        reduce_rows(g)
+    lax.fori_loop(0, KV_HEADS, own_grads, 0)
+
     for g in range(KV_HEADS):
         for d in range(1, n_rep):
             slot = rbuf.at[g, rep_at(n_rep - d)]
             pltpu.make_async_copy(slot, slot, r_rsem.at[g, d - 1]).wait()
-        total = rbuf[g, 0]
-        for i in range(1, n_rep):
-            total = total + rbuf[g, i]
-        pk_out[:, g * HEAD_DIM:(g + 1) * HEAD_DIM] = total[0]
-        pv_out[:, g * HEAD_DIM:(g + 1) * HEAD_DIM] = total[1]
+        for first, out in ((0, pk_out), (1, pv_out)):
+            total = rbuf[g, first]
+            for i in range(first + 2, n_rep, 2):
+                total = total + rbuf[g, i]
+            out[:, g * HEAD_DIM:(g + 1) * HEAD_DIM] = total
     for d in range(1, n_fsdp):
         gather(d).wait_send()
     for g in range(KV_HEADS):
+        swap(g).wait_send()
         for d in range(1, n_fsdp):
             scatter(g, d).wait_send()
         for d in range(1, n_rep):
@@ -197,7 +251,7 @@
     any_ = pl.BlockSpec(memory_space=pl.ANY)
     vmem = pl.BlockSpec(memory_space=pltpu.VMEM)
     dma = pltpu.SemaphoreType.DMA
-    piece = (2, pre_rows, HEAD_DIM)
+    piece = (pre_rows, HEAD_DIM)
     held = pl.pallas_call(
         functools.partial(kernel, n_rep, n_fsdp),
         out_shape=(
@@ -215,9 +269,15 @@
             pltpu.VMEM((KV_HEADS, rows, WIDTH), BF16),
             pltpu.VMEM((KV_HEADS, rows, HEAD_DIM), BF16),
             pltpu.VMEM((KV_HEADS, rows, HEAD_DIM), BF16),
-            pltpu.VMEM((n_fsdp, KV_HEADS) + piece, BF16),
-            pltpu.VMEM((keys, GROUP * rows), BF16),
-            pltpu.VMEM((keys, GROUP * rows), BF16),
+            pltpu.VMEM((n_fsdp, KV_HEADS, 2) + piece, BF16),
+            pltpu.VMEM((KV_HEADS, rows, GROUP * rows), F32),
+            pltpu.VMEM((KV_HEADS, rows, GROUP * rows), F32),
+            pltpu.VMEM((KV_HEADS, GROUP * rows, HEAD_DIM), BF16),
+            pltpu.VMEM((KV_HEADS, 8, GROUP * rows), F32),
+            pltpu.VMEM((KV_HEADS, keys, GROUP * rows), BF16),
+            pltpu.VMEM((KV_HEADS, keys, GROUP * rows), BF16),
+            pltpu.VMEM((KV_HEADS, 2, n_fsdp) + piece, F32),
+            pltpu.VMEM((KV_HEADS, n_fsdp) + piece, F32),
             pltpu.VMEM((KV_HEADS, n_fsdp) + piece, F32),
             pltpu.VMEM((KV_HEADS, n_fsdp) + piece, F32),
             pltpu.VMEM((KV_HEADS, n_rep) + piece, F32),
@@ -225,6 +285,8 @@
             dma((2, KV_HEADS)),
             dma((n_fsdp - 1,)),
             dma((n_fsdp - 1,)),
+            dma((KV_HEADS,)),
+            dma((KV_HEADS,)),
             dma((KV_HEADS, n_fsdp - 1)),
             dma((KV_HEADS, n_fsdp - 1)),
             dma((KV_HEADS, n_rep - 1)),

time: 28 us -> 24.8 us (0.89)
  Pallas kernels: 26.5 us -> 23.3 us
    pallas_call x1, Pallas kernels: 25.4 us -> 22.2 us  [on_device(): pl.pallas_call(functools.partial(kernel, n_rep, n_fsdp), out_shape=(pltpu...]
where the time goes in v3:
time: 24.8 us; the launch traced here: 24.6 us
  Pallas kernels  23.3 us (94%)
  between operations  1.29 us (5%)
    pallas_call x1, Pallas kernels, on_device(): pl.pallas_call(functools.partial(kernel, n_rep, n_fsdp), out_shape=(pltpu...  22.2 us
    pallas_call x1, Pallas kernels, on_device(): pl.pallas_call(write_out, out_shape=tuple((jax.ShapeDtypeStruct(x.shape,...  1.1 us

profile of v3, /device:TPU:0, one launch (start us, length us, event | category | flops | bytes accessed | tf_op | source)
XLA Modules:
  0.0 24.6 jit_solution(10635468965176942864)
XLA Ops:
  1.3 22.2 %shard_map.119 = (bf16[128,4096]{1,0:T(8,128)(2,1)S(1)}, bf16[128,512]{1,0:T(8,128)(2,1)S(1)}, bf16[128,512]{1,0:T(8,128)(2,1)S(1)}, f32[16,512]{1,0:T(8,128)S(1)}, f32[16,512]{1,0:T(8,128)S(1)}) custom-call(bf16[128,4096]{1,0:T(8,128)(2,1)} %q_hbm.1, bf16[128,512]{1,0:T(8,128)(2,1)} %k_hbm.1, bf16[128,512]{1,0:T(8,128)(2,1)} %v_hbm.1, ...), custom_call_target="tpu_custom_call" | custom-call | tf_op jit(solution)/shard_map/pallas_call | solution.py:255
  23.5 1.1 %shard_map.120 = (bf16[128,4096]{1,0:T(8,128)(2,1)}, bf16[128,512]{1,0:T(8,128)(2,1)}, bf16[128,512]{1,0:T(8,128)(2,1)}, f32[16,512]{1,0:T(8,128)}, f32[16,512]{1,0:T(8,128)}) custom-call(bf16[128,4096]{1,0:T(8,128)(2,1)S(1)} %get-tuple-element.10.refs_0_, bf16[128,512]{1,0:T(8,128)(2,1)S(1)} %get-tuple-element.11.refs_1_, ...), custom_call_target="tpu_custom_call" | custom-call | tf_op jit(solution)/shard_map/pallas_call | solution.py:297
